TPU v7x, 256 devices: a whole 4x4x8 slice. The times are simulated.
256 devices in a mesh: harm: 64 (over y, z, core), node: 4 (over x).
Axes of the slice: x: 4, y: 4, z: 8, core: 2. Of those that a mesh axis runs over, the one named last changes fastest.
Arguments:
- state: float32 [2, 128, 512, 128], P(None, 'harm', 'node'), may hold values from -0.6 to 0.6
- source: float32 [2, 128, 512, 128], P(None, 'harm', 'node'), may hold values from -6 to 6
- capacity: float32 [512, 128], P('node'), may hold values from 0.05 to 0.5
- row_shift: int32 [512], P('node'), may hold values from 0 to 3
- device_type: int32 [512, 128], P('node'), may hold values from 0 to 3
- device_table: float32 [3, 4], replicated, may hold values from 0.5 to 2
- precond: float32 [2, 128, 128, 128], P(None, 'harm'), may hold values from -1 to 1, as said below
Outputs:
- update: float32 [2, 128, 512, 128], P(None, 'harm', 'node')
- resid: float32 [2, 128, 512, 128], P(None, 'harm', 'node')
Inputs may be any that keep to these rules, and one draw needn't show every extreme that they name: precond[0, k] is 1/6 on the diagonal plus a full-rank fluctuation; precond[1, k] is a full-rank fluctuation.
All inputs are finite; a program needn't handle non-finite values.
Results may differ from a plain program's by a relative error of at most 0.00011.
Values sent between devices are 32-bit elements; how exact they have to be, the bound alone decides.
A program may use at most 64 MiB of HBM per device.

v0:
```python
import functools
import jax
import jax.numpy as jnp
from jax import lax
from jax.sharding import Mesh
from jax.sharding import PartitionSpec as P

ITERS = 3
TYPES = 4
SHIFTS = 4
HARM = ("harm_0", "harm_1", "harm_2")
HARM_NODE = ("harm_0", "harm_1", "harm_2", "node")
omega_step = 0.05
top = lax.Precision.HIGHEST


def extended(cells, sides, width):
    for axis, dim in sides:
        count = lax.axis_size(axis)
        ends = count - 1
        head = lax.slice_in_dim(cells, 0, width, axis=dim)
        tail = lax.slice_in_dim(cells, cells.shape[dim] - width, cells.shape[dim], axis=dim)
        cells = jnp.concatenate(
            [
                lax.ppermute(tail, axis, [(i, (i + 1) % count) for i in range(ends)]),
                cells,
                lax.ppermute(head, axis, [((i + 1) % count, i) for i in range(ends)]),
            ],
            axis=dim,
        )
    return cells


def by_axis(shard, axes):
    return functools.reduce(lax.psum, axes, shard)


def small_solve(gram, right):
    lower = jnp.linalg.cholesky(gram)
    order = gram.shape[0]
    forward = []
    for column in range(order):
        value = right[column]
        for member in range(column):
            value = value - lower[column, member] * forward[member]
        forward.append(value / lower[column, column])
    result = [None] * order
    for column in reversed(range(order)):
        value = forward[column]
        for member in range(column + 1, order):
            value = value - lower[member, column] * result[member]
        result[column] = value / lower[column, column]
    return result


def tables(harmonics, samples):
    waves = jnp.arange(harmonics, dtype=jnp.int32)
    moments = jnp.arange(samples, dtype=jnp.int32)
    phase = (moments[:, None] * waves[None, :] % samples).astype(jnp.float32) * (
        2.0 * jnp.pi / samples
    )
    cosine = jnp.cos(phase)
    sine = jnp.sin(phase)
    inverse = jnp.concatenate([cosine, -sine], axis=1)
    weights = jnp.where(waves == 0, 1.0, 2.0).astype(jnp.float32) / samples
    forward = jnp.concatenate([cosine.T * weights[:, None], -sine.T * weights[:, None]], axis=0)
    return (inverse, forward)


def stencil(field, above, below, capacity, shifts, waves):
    left_side = jnp.roll(field, 1, axis=3)
    right_side = jnp.roll(field, -1, axis=3)
    skewed = jnp.zeros_like(field)
    for amount in range(SHIFTS):
        picked = (shifts == amount).astype(jnp.float32)[None, None, :, None]
        skewed = skewed + picked * jnp.roll(above, -amount, axis=3)
    result = 4.0 * field - left_side - right_side - skewed - below
    reactive = omega_step * waves.astype(jnp.float32)[:, None, None] * capacity[None]
    return result + jnp.stack([-reactive * field[1], reactive * field[0]])


def precondition(field, blocks):
    real_part = jnp.einsum("krd,kcd->krc", field[0], blocks[0], precision=top) - jnp.einsum(
        "krd,kcd->krc", field[1], blocks[1], precision=top
    )
    imag_part = jnp.einsum("krd,kcd->krc", field[0], blocks[1], precision=top) + jnp.einsum(
        "krd,kcd->krc", field[1], blocks[0], precision=top
    )
    return jnp.stack([real_part, imag_part])


def body(state, source, capacity, row_shift, device_type, device_table, precond):
    groups = lax.axis_size(HARM)
    place = lax.axis_index(HARM)
    local_harm = state.shape[1]
    block_rows = state.shape[2]
    columns = state.shape[3]
    harmonics = local_harm * groups
    samples = 2 * harmonics
    own_rows = block_rows // groups
    inverse, forward = tables(harmonics, samples)
    kinds = lax.dynamic_slice_in_dim(device_type, place * own_rows, own_rows, 0).reshape(-1)
    params = jnp.zeros((3, kinds.shape[0]), jnp.float32)
    for member in range(TYPES):
        params = (
            params
            + (kinds == member).astype(jnp.float32)[None, :] * device_table[:, member][:, None]
        )
    linear, amplitude, slope = (params[0], params[1], params[2])

    def time_of(spectrum):
        return jnp.dot(
            inverse,
            spectrum.reshape(2 * harmonics, -1),
            precision=top,
            preferred_element_type=jnp.float32,
        )

    def spectrum_of(signal):
        return jnp.dot(forward, signal, precision=top, preferred_element_type=jnp.float32).reshape(
            2, harmonics, own_rows, columns
        )

    def currents(spectrum):
        voltage = time_of(spectrum)
        bent = jnp.tanh(slope * voltage)
        flow = linear * voltage + amplitude * bent
        slopes_now = linear + amplitude * slope * (1.0 - bent * bent)
        return (spectrum_of(flow), slopes_now)

    field_state, field_source = (state, source)
    waves = place * local_harm + jnp.arange(local_harm, dtype=jnp.int32)

    def sides(field):
        padded = extended(field, (("node", 2),), 1)
        return (padded[:, :, :-2], padded[:, :, 2:])

    def across(field, local):
        moved = lax.all_to_all(field, HARM, split_axis=2, concat_axis=1, tiled=True)
        result, extra = local(moved)
        return (lax.all_to_all(result, HARM, split_axis=1, concat_axis=2, tiled=True), extra)

    def operator(field):
        above, below = sides(field)
        return stencil(field, above, below, capacity, row_shift, waves)

    spec_flow, slopes = across(field_state, currents)
    resid = operator(field_state) + spec_flow - field_source

    def linear_part(spectrum):
        return (spectrum_of(slopes * time_of(spectrum)), slopes)

    start = -resid
    beta = jnp.sqrt(by_axis(jnp.sum(start * start), HARM_NODE))
    basis = [start / beta]
    directions = []
    columns_h = []
    for iteration in range(ITERS):
        direction = precondition(basis[iteration], precond)
        directions.append(direction)
        coupled, unused = across(direction, linear_part)
        image = operator(direction) + coupled
        locals_dot = jnp.stack([jnp.sum(basis[member] * image) for member in range(iteration + 1)])
        totals, square = (
            by_axis(locals_dot, HARM_NODE),
            by_axis(jnp.sum(image * image), HARM_NODE),
        )
        heights = [totals[member] for member in range(iteration + 1)]
        for earlier in range(iteration + 1):
            image = image - heights[earlier] * basis[earlier]
        length = jnp.sqrt(square - jnp.sum(totals * totals))
        columns_h.append(
            jnp.stack(heights + [length] + [jnp.zeros((), jnp.float32)] * (ITERS - 1 - iteration))
        )
        if iteration + 1 < ITERS:
            basis.append(image / length)
    hess = jnp.stack(columns_h, axis=1)
    gram = jnp.dot(hess.T, hess, precision=top)
    coeffs = small_solve(gram, beta * hess[0])
    update = jnp.zeros_like(field_state)
    for iteration in range(ITERS):
        update = update + coeffs[iteration] * directions[iteration]
    return (update, resid)


def solution(mesh):
    finer = Mesh(
        mesh.devices.reshape(4, 8, 2, mesh.shape["node"]), ("harm_0", "harm_1", "harm_2", "node")
    )
    return jax.shard_map(
        body,
        mesh=finer,
        in_specs=(
            P(None, HARM, "node", None),
            P(None, HARM, "node", None),
            P("node", None),
            P("node"),
            P("node", None),
            P(),
            P(None, HARM, None, None),
        ),
        out_specs=(P(None, HARM, "node", None), P(None, HARM, "node", None)),
        check_vma=False,
    )
```

profile of v0, /device:TPU:2, one launch (start us, length us, event | category | flops | bytes accessed | tf_op | source)
XLA Modules:
  0.0 376.9 jit_solution(4590156179275727498)
XLA Ops:
  9.1 12.2 %all-to-all-start = ((f32[2,2,128,128]{3,1,0,2:T(2,128)}), f32[2,2,128,128]{3,1,0,2:T(2,128)S(1)}, u32[]{:S(2)}, u32[]{:S(2)}) async-start(f32[2,2,128,128]{3,1,0,2:T(2,128)} %copy.23), calls=%async_computation | async-start | bytes 524288 | tf_op jit(solution)/shard_map/all_to_all | solution.py:139
  24.8 8.5 %all-to-all-done = f32[2,2,128,128]{3,1,0,2:T(2,128)S(1)} async-done(((f32[2,2,128,128]{3,1,0,2:T(2,128)}), f32[2,2,128,128]{3,1,0,2:T(2,128)S(1)}, u32[]{:S(2)}, u32[]{:S(2)}) %all-to-all-start) | async-done | bytes 262176 | tf_op jit(solution)/shard_map/all_to_all | solution.py:139
  35.2 6.0 %all-to-all-start.1 = ((f32[2,128,2,128]{3,2,0,1:T(2,128)}), f32[2,128,2,128]{3,2,0,1:T(2,128)S(1)}, u32[]{:S(2)}, u32[]{:S(2)}) async-start(f32[2,128,2,128]{3,2,0,1:T(2,128)} %copy.25), calls=%async_computation.1 | async-start | bytes 524288 | tf_op jit(solution)/shard_map/all_to_all | solution.py:141
  42.3 10.9 %all-to-all-done.1 = f32[2,128,2,128]{3,2,0,1:T(2,128)S(1)} async-done(((f32[2,128,2,128]{3,2,0,1:T(2,128)}), f32[2,128,2,128]{3,2,0,1:T(2,128)S(1)}, u32[]{:S(2)}, u32[]{:S(2)}) %all-to-all-start.1) | async-done | bytes 262176 | tf_op jit(solution)/shard_map/all_to_all | solution.py:141
  56.3 10.9 %psum.196 = f32[]{:T(128)} all-reduce(f32[]{:T(128)} %get-tuple-element.41), channel_id=1, replica_groups=mesh['harm_0'=4,'harm_1'=8,'harm_2'=2,'node'=4] {'harm_0'}, use_global_device_ids=true, to_apply=%region_1.2 | all-reduce | flops 1 | bytes 8 | tf_op jit(solution)/shard_map/psum | solution.py:35
  67.2 15.5 %psum.197 = f32[]{:T(128)} all-reduce(f32[]{:T(128)} %psum.196), channel_id=1, replica_groups=mesh['harm_0'=4,'harm_1'=8,'harm_2'=2,'node'=4] {'harm_1'}, use_global_device_ids=true, to_apply=%region_2.3 | all-reduce | flops 1 | bytes 8 | tf_op jit(solution)/shard_map/psum | solution.py:35
  85.8 9.2 %psum.199 = f32[]{:T(128)} all-reduce(f32[]{:T(128)} %psum.198), channel_id=1, replica_groups=mesh['harm_0'=4,'harm_1'=8,'harm_2'=2,'node'=4] {'node'}, use_global_device_ids=true, to_apply=%region_4.5 | all-reduce | flops 1 | bytes 8 | tf_op jit(solution)/shard_map/psum | solution.py:35
  99.2 5.6 %all-to-all-start.2 = ((f32[2,2,128,128]{3,1,0,2:T(2,128)}), f32[2,2,128,128]{3,1,0,2:T(2,128)S(1)}, u32[]{:S(2)}, u32[]{:S(2)}) async-start(f32[2,2,128,128]{3,1,0,2:T(2,128)} %copy.27), calls=%async_computation.2 | async-start | bytes 524288 | tf_op jit(solution)/shard_map/all_to_all | solution.py:139
  105.0 11.8 %all-to-all-done.2 = f32[2,2,128,128]{3,1,0,2:T(2,128)S(1)} async-done(((f32[2,2,128,128]{3,1,0,2:T(2,128)}), f32[2,2,128,128]{3,1,0,2:T(2,128)S(1)}, u32[]{:S(2)}, u32[]{:S(2)}) %all-to-all-start.2) | async-done | bytes 262176 | tf_op jit(solution)/shard_map/all_to_all | solution.py:139
  118.7 6.0 %all-to-all-start.3 = ((f32[2,128,2,128]{3,2,0,1:T(2,128)}), f32[2,128,2,128]{3,2,0,1:T(2,128)S(1)}, u32[]{:S(2)}, u32[]{:S(2)}) async-start(f32[2,128,2,128]{3,2,0,1:T(2,128)} %copy.29), calls=%async_computation.3 | async-start | bytes 524288 | tf_op jit(solution)/shard_map/all_to_all | solution.py:141
  140.1 11.0 %all-reduce.8 = (f32[]{:T(128)}, f32[1]{0:T(128)}) all-reduce(f32[]{:T(128)} %get-tuple-element.10, f32[1]{0:T(128)} %bitcast.26), channel_id=1, replica_groups=mesh['harm_0'=4,'harm_1'=8,'harm_2'=2,'node'=4] {'harm_0'}, use_global_device_ids=true, to_apply=%region_11.12 | all-reduce | flops 2 | bytes 16 | tf_op jit(solution)/shard_map/psum | solution.py:35
  151.1 17.0 %all-reduce.2 = (f32[]{:T(128)}, f32[1]{0:T(128)}) all-reduce(f32[]{:T(128)} %get-tuple-element.31, f32[1]{0:T(128)} %get-tuple-element.32), channel_id=1, replica_groups=mesh['harm_0'=4,'harm_1'=8,'harm_2'=2,'node'=4] {'harm_1'}, use_global_device_ids=true, to_apply=%region_12.13 | all-reduce | flops 2 | bytes 16 | tf_op jit(solution)/shard_map/psum | solution.py:35
  171.3 9.3 %all-reduce.5 = (f32[]{:T(128)}, f32[1]{0:T(128)}) all-reduce(f32[]{:T(128)} %get-tuple-element.37, f32[1]{0:T(128)} %get-tuple-element.38), channel_id=1, replica_groups=mesh['harm_0'=4,'harm_1'=8,'harm_2'=2,'node'=4] {'node'}, use_global_device_ids=true, to_apply=%region_14.15 | all-reduce | flops 2 | bytes 16 | tf_op jit(solution)/shard_map/psum | solution.py:35
  191.3 11.8 %all-to-all-done.4 = f32[2,2,128,128]{3,1,0,2:T(2,128)S(1)} async-done(((f32[2,2,128,128]{3,1,0,2:T(2,128)}), f32[2,2,128,128]{3,1,0,2:T(2,128)S(1)}, u32[]{:S(2)}, u32[]{:S(2)}) %all-to-all-start.4) | async-done | bytes 262176 | tf_op jit(solution)/shard_map/all_to_all | solution.py:139
  205.0 6.3 %all-to-all-start.5 = ((f32[2,128,2,128]{3,2,0,1:T(2,128)}), f32[2,128,2,128]{3,2,0,1:T(2,128)}, u32[]{:S(2)}, u32[]{:S(2)}) async-start(f32[2,128,2,128]{3,2,0,1:T(2,128)} %copy.34), calls=%async_computation.5 | async-start | bytes 524288 | tf_op jit(solution)/shard_map/all_to_all | solution.py:141
  229.5 11.1 %all-reduce.7 = (f32[]{:T(128)}, f32[2]{0:T(128)S(1)}) all-reduce(f32[]{:T(128)} %get-tuple-element.7, f32[2]{0:T(128)S(1)} %pad_maximum_fusion.22), channel_id=1, replica_groups=mesh['harm_0'=4,'harm_1'=8,'harm_2'=2,'node'=4] {'harm_0'}, use_global_device_ids=true, to_apply=%region_22.23 | all-reduce | flops 3 | bytes 24 | tf_op jit(solution)/shard_map/psum | solution.py:35
  240.6 17.5 %all-reduce.1 = (f32[]{:T(128)}, f32[2]{0:T(128)S(1)}) all-reduce(f32[]{:T(128)} %get-tuple-element.29, f32[2]{0:T(128)S(1)} %get-tuple-element.30), channel_id=1, replica_groups=mesh['harm_0'=4,'harm_1'=8,'harm_2'=2,'node'=4] {'harm_1'}, use_global_device_ids=true, to_apply=%region_23.24 | all-reduce | flops 3 | bytes 24 | tf_op jit(solution)/shard_map/psum | solution.py:35
  261.2 8.0 %all-reduce.4 = (f32[]{:T(128)}, f32[2]{0:T(128)S(1)}) all-reduce(f32[]{:T(128)} %get-tuple-element.35, f32[2]{0:T(128)S(1)} %get-tuple-element.36), channel_id=1, replica_groups=mesh['harm_0'=4,'harm_1'=8,'harm_2'=2,'node'=4] {'node'}, use_global_device_ids=true, to_apply=%region_25.26 | all-reduce | flops 3 | bytes 24 | tf_op jit(solution)/shard_map/psum | solution.py:35
  276.6 5.8 %all-to-all-start.6 = ((f32[2,2,128,128]{3,1,0,2:T(2,128)}), f32[2,2,128,128]{3,1,0,2:T(2,128)S(1)}, u32[]{:S(2)}, u32[]{:S(2)}) async-start(f32[2,2,128,128]{3,1,0,2:T(2,128)} %copy.37), calls=%async_computation.6 | async-start | bytes 524288 | tf_op jit(solution)/shard_map/all_to_all | solution.py:139
  284.6 9.8 %all-to-all-done.6 = f32[2,2,128,128]{3,1,0,2:T(2,128)S(1)} async-done(((f32[2,2,128,128]{3,1,0,2:T(2,128)}), f32[2,2,128,128]{3,1,0,2:T(2,128)S(1)}, u32[]{:S(2)}, u32[]{:S(2)}) %all-to-all-start.6) | async-done | bytes 262176 | tf_op jit(solution)/shard_map/all_to_all | solution.py:139
  296.2 6.3 %all-to-all-start.7 = ((f32[2,128,2,128]{3,2,0,1:T(2,128)}), f32[2,128,2,128]{3,2,0,1:T(2,128)}, u32[]{:S(2)}, u32[]{:S(2)}) async-start(f32[2,128,2,128]{3,2,0,1:T(2,128)} %copy.39), calls=%async_computation.7 | async-start | bytes 524288 | tf_op jit(solution)/shard_map/all_to_all | solution.py:141
  320.5 10.9 %all-reduce.6 = (f32[]{:T(128)}, f32[3]{0:T(128)S(1)}) all-reduce(f32[]{:T(128)} %get-tuple-element.3, f32[3]{0:T(128)S(1)} %pad_maximum_fusion.23), channel_id=1, replica_groups=mesh['harm_0'=4,'harm_1'=8,'harm_2'=2,'node'=4] {'harm_0'}, use_global_device_ids=true, to_apply=%region_35.36 | all-reduce | flops 4 | bytes 32 | tf_op jit(solution)/shard_map/psum | solution.py:35
  331.4 16.1 %all-reduce = (f32[]{:T(128)}, f32[3]{0:T(128)S(1)}) all-reduce(f32[]{:T(128)} %get-tuple-element.27, f32[3]{0:T(128)S(1)} %get-tuple-element.28), channel_id=1, replica_groups=mesh['harm_0'=4,'harm_1'=8,'harm_2'=2,'node'=4] {'harm_1'}, use_global_device_ids=true, to_apply=%region_36.37 | all-reduce | flops 4 | bytes 32 | tf_op jit(solution)/shard_map/psum | solution.py:35
  350.6 10.2 %all-reduce.3 = (f32[]{:T(128)}, f32[3]{0:T(128)S(1)}) all-reduce(f32[]{:T(128)} %get-tuple-element.33, f32[3]{0:T(128)S(1)} %get-tuple-element.34), channel_id=1, replica_groups=mesh['harm_0'=4,'harm_1'=8,'harm_2'=2,'node'=4] {'node'}, use_global_device_ids=true, to_apply=%region_38.39 | all-reduce | flops 4 | bytes 32 | tf_op jit(solution)/shard_map/psum | solution.py:35
  (193 shorter events, 112.7 us)
Async XLA Ops:
  1.4 23.2 %collective-permute-start = (f32[2,2,1,128]{3,2,1,0:T(1,128)S(1)}, f32[2,2,1,128]{3,2,1,0:T(1,128)S(1)}, u32[]{:S(2)}, u32[]{:S(2)}) collective-permute-start(f32[2,2,1,128]{3,2,1,0:T(1,128)S(1)} %get-tuple-element.69), channel_id=1, source_target_pairs={{0,1},{1,2},{2,3},{4,5},{5,6},{6,7},{8,9},{9,10},{10,11},{12,13},{... | collective-permute-start | bytes 6152 | tf_op jit(solution)/shard_map/ppermute | solution.py:25
  4.8 48.5 %collective-permute-start.1 = (f32[2,2,1,128]{3,2,1,0:T(1,128)S(1)}, f32[2,2,1,128]{3,2,1,0:T(1,128)S(1)}, u32[]{:S(2)}, u32[]{:S(2)}) collective-permute-start(f32[2,2,1,128]{3,2,1,0:T(1,128)S(1)} %get-tuple-element.70), channel_id=1, source_target_pairs={{1,0},{2,1},{3,2},{5,4},{6,5},{7,6},{9,8},{10,9},{11,10},{13,12},{... | collective-permute-start | bytes 6152 | tf_op jit(solution)/shard_map/ppermute | solution.py:27
  9.1 12.3 %copy-start.20 = (f32[3,4]{1,0:T(4,128)S(1)}, f32[3,4]{1,0:T(4,128)}, u32[]{:S(2)}) copy-start(f32[3,4]{1,0:T(4,128)} %param.12) | copy-start | bytes 148
  9.1 24.2 %all-to-all-start = ((f32[2,2,128,128]{3,1,0,2:T(2,128)}), f32[2,2,128,128]{3,1,0,2:T(2,128)S(1)}, u32[]{:S(2)}, u32[]{:S(2)}) async-start(f32[2,2,128,128]{3,1,0,2:T(2,128)} %copy.23), calls=%async_computation | async-start | bytes 524288 | tf_op jit(solution)/shard_map/all_to_all | solution.py:139
  21.3 1.6 copy-start
  35.2 18.0 %all-to-all-start.1 = ((f32[2,128,2,128]{3,2,0,1:T(2,128)}), f32[2,128,2,128]{3,2,0,1:T(2,128)S(1)}, u32[]{:S(2)}, u32[]{:S(2)}) async-start(f32[2,128,2,128]{3,2,0,1:T(2,128)} %copy.25), calls=%async_computation.1 | async-start | bytes 524288 | tf_op jit(solution)/shard_map/all_to_all | solution.py:141
  56.3 259.3 %copy-start.1 = (f32[2,2,128,128]{3,2,1,0:T(8,128)}, f32[2,2,128,128]{3,2,1,0:T(8,128)S(1)}, u32[]{:S(2)}) copy-start(f32[2,2,128,128]{3,2,1,0:T(8,128)S(1)} %get-tuple-element.42) | copy-start | bytes 786436
  99.2 17.6 %all-to-all-start.2 = ((f32[2,2,128,128]{3,1,0,2:T(2,128)}), f32[2,2,128,128]{3,1,0,2:T(2,128)S(1)}, u32[]{:S(2)}, u32[]{:S(2)}) async-start(f32[2,2,128,128]{3,1,0,2:T(2,128)} %copy.27), calls=%async_computation.2 | async-start | bytes 524288 | tf_op jit(solution)/shard_map/all_to_all | solution.py:139
  118.7 18.0 %all-to-all-start.3 = ((f32[2,128,2,128]{3,2,0,1:T(2,128)}), f32[2,128,2,128]{3,2,0,1:T(2,128)S(1)}, u32[]{:S(2)}, u32[]{:S(2)}) async-start(f32[2,128,2,128]{3,2,0,1:T(2,128)} %copy.29), calls=%async_computation.3 | async-start | bytes 524288 | tf_op jit(solution)/shard_map/all_to_all | solution.py:141
  124.7 7.0 %collective-permute-start.2 = (f32[2,2,1,128]{3,2,1,0:T(1,128)S(1)}, f32[2,2,1,128]{3,2,1,0:T(1,128)S(1)}, u32[]{:S(2)}, u32[]{:S(2)}) collective-permute-start(f32[2,2,1,128]{3,2,1,0:T(1,128)S(1)} %get-tuple-element.61), channel_id=1, source_target_pairs={{0,1},{1,2},{2,3},{4,5},{5,6},{6,7},{8,9},{9,10},{10,11},{12,13},{... | collective-permute-start | bytes 6152 | tf_op jit(solution)/shard_map/ppermute | solution.py:25
  128.7 8.2 %collective-permute-start.3 = (f32[2,2,1,128]{3,2,1,0:T(1,128)S(1)}, f32[2,2,1,128]{3,2,1,0:T(1,128)S(1)}, u32[]{:S(2)}, u32[]{:S(2)}) collective-permute-start(f32[2,2,1,128]{3,2,1,0:T(1,128)S(1)} %get-tuple-element.62), channel_id=1, source_target_pairs={{1,0},{2,1},{3,2},{5,4},{6,5},{7,6},{9,8},{10,9},{11,10},{13,12},{... | collective-permute-start | bytes 6152 | tf_op jit(solution)/shard_map/ppermute | solution.py:27
  185.6 17.6 %all-to-all-start.4 = ((f32[2,2,128,128]{3,1,0,2:T(2,128)}), f32[2,2,128,128]{3,1,0,2:T(2,128)S(1)}, u32[]{:S(2)}, u32[]{:S(2)}) async-start(f32[2,2,128,128]{3,1,0,2:T(2,128)} %copy.32), calls=%async_computation.4 | async-start | bytes 524288 | tf_op jit(solution)/shard_map/all_to_all | solution.py:139
  205.0 18.1 %all-to-all-start.5 = ((f32[2,128,2,128]{3,2,0,1:T(2,128)}), f32[2,128,2,128]{3,2,0,1:T(2,128)}, u32[]{:S(2)}, u32[]{:S(2)}) async-start(f32[2,128,2,128]{3,2,0,1:T(2,128)} %copy.34), calls=%async_computation.5 | async-start | bytes 524288 | tf_op jit(solution)/shard_map/all_to_all | solution.py:141
  211.3 6.8 %collective-permute-start.4 = (f32[2,2,1,128]{3,2,1,0:T(1,128)S(1)}, f32[2,2,1,128]{3,2,1,0:T(1,128)S(1)}, u32[]{:S(2)}, u32[]{:S(2)}) collective-permute-start(f32[2,2,1,128]{3,2,1,0:T(1,128)S(1)} %get-tuple-element.55), channel_id=1, source_target_pairs={{0,1},{1,2},{2,3},{4,5},{5,6},{6,7},{8,9},{9,10},{10,11},{12,13},{... | collective-permute-start | bytes 6152 | tf_op jit(solution)/shard_map/ppermute | solution.py:25
  214.4 10.0 %collective-permute-start.5 = (f32[2,2,1,128]{3,2,1,0:T(1,128)S(1)}, f32[2,2,1,128]{3,2,1,0:T(1,128)S(1)}, u32[]{:S(2)}, u32[]{:S(2)}) collective-permute-start(f32[2,2,1,128]{3,2,1,0:T(1,128)S(1)} %get-tuple-element.56), channel_id=1, source_target_pairs={{1,0},{2,1},{3,2},{5,4},{6,5},{7,6},{9,8},{10,9},{11,10},{13,12},{... | collective-permute-start | bytes 6152 | tf_op jit(solution)/shard_map/ppermute | solution.py:27
  223.1 1.3 copy-start.9
  223.1 1.3 copy-start.10
  276.6 17.8 %all-to-all-start.6 = ((f32[2,2,128,128]{3,1,0,2:T(2,128)}), f32[2,2,128,128]{3,1,0,2:T(2,128)S(1)}, u32[]{:S(2)}, u32[]{:S(2)}) async-start(f32[2,2,128,128]{3,1,0,2:T(2,128)} %copy.37), calls=%async_computation.6 | async-start | bytes 524288 | tf_op jit(solution)/shard_map/all_to_all | solution.py:139
  296.2 18.1 %all-to-all-start.7 = ((f32[2,128,2,128]{3,2,0,1:T(2,128)}), f32[2,128,2,128]{3,2,0,1:T(2,128)}, u32[]{:S(2)}, u32[]{:S(2)}) async-start(f32[2,128,2,128]{3,2,0,1:T(2,128)} %copy.39), calls=%async_computation.7 | async-start | bytes 524288 | tf_op jit(solution)/shard_map/all_to_all | solution.py:141
  302.6 6.7 %collective-permute-start.6 = (f32[2,2,1,128]{3,2,1,0:T(1,128)S(1)}, f32[2,2,1,128]{3,2,1,0:T(1,128)S(1)}, u32[]{:S(2)}, u32[]{:S(2)}) collective-permute-start(f32[2,2,1,128]{3,2,1,0:T(1,128)S(1)} %get-tuple-element.49), channel_id=1, source_target_pairs={{0,1},{1,2},{2,3},{4,5},{5,6},{6,7},{8,9},{9,10},{10,11},{12,13},{... | collective-permute-start | bytes 6152 | tf_op jit(solution)/shard_map/ppermute | solution.py:25
  305.7 10.0 %collective-permute-start.7 = (f32[2,2,1,128]{3,2,1,0:T(1,128)S(1)}, f32[2,2,1,128]{3,2,1,0:T(1,128)S(1)}, u32[]{:S(2)}, u32[]{:S(2)}) collective-permute-start(f32[2,2,1,128]{3,2,1,0:T(1,128)S(1)} %get-tuple-element.50), channel_id=1, source_target_pairs={{1,0},{2,1},{3,2},{5,4},{6,5},{7,6},{9,8},{10,9},{11,10},{13,12},{... | collective-permute-start | bytes 6152 | tf_op jit(solution)/shard_map/ppermute | solution.py:27
  311.7 3.9 %copy-start.19 = (f32[1,2,128,128]{3,2,1,0:T(8,128)S(1)}, f32[1,2,128,128]{3,2,1,0:T(8,128)}, u32[]{:S(2)}) copy-start(f32[1,2,128,128]{3,2,1,0:T(8,128)} %get-tuple-element.72) | copy-start | bytes 393220
  314.4 1.3 copy-start.5
  314.4 1.3 copy-start.6
  (15 other events, 14.4 us)
where the time goes:
time: 379 us; the launch traced here: 377 us
  blocking collectives  159 us (42%)
  starting transfers between devices  77.5 us (20%)
  waiting for transfers between devices  55.9 us (15%)
  local copies, waits for them, and re-layouts  31.7 us (8%)
  other arithmetic  28.6 us (8%)
  between operations  16.3 us (4%)
  matrix products  7.83 us (2%)
    psum x16, blocking collectives, by_axis(): return functools.reduce(lax.psum, axes, shard)  159 us
    all_to_all x4, waiting for transfers between devices, across(): moved = lax.all_to_all(field, HARM, split_axis=2, concat_axis=1, tiled=True)  42 us
    all_to_all x4, starting transfers between devices, across(): moved = lax.all_to_all(field, HARM, split_axis=2, concat_axis=1, tiled=True)  29.3 us
    all_to_all x4, starting transfers between devices, across(): lax.all_to_all(result, HARM, split_axis=1, concat_axis=2, tiled=True)  24.6 us
    all_to_all x4, waiting for transfers between devices, across(): lax.all_to_all(result, HARM, split_axis=1, concat_axis=2, tiled=True)  13.9 us
    slice x18, local copies, waits for them, and re-layouts, stencil(): skewed = skewed + picked * jnp.roll(above, -amount, axis=3)  12 us
    ppermute x4, starting transfers between devices, extended(): lax.ppermute(head, axis, [((i + 1) % count, i) for i in range(ends)])  11.8 us
    ppermute x4, starting transfers between devices, extended(): lax.ppermute(tail, axis, [(i, (i + 1) % count) for i in range(ends)])  11.7 us
  transfers between devices with their start and end apart: 16, of which 8 were waited for; matrix products, arithmetic and copies ran while one was open for 7% of the time, Pallas kernels for 0%

commit v1 on v0

--- a/solution.py
+++ b/solution.py
@@ -138,7 +138,15 @@
     def across(field, local):
         moved = lax.all_to_all(field, HARM, split_axis=2, concat_axis=1, tiled=True)
         result, extra = local(moved)
-        return (lax.all_to_all(result, HARM, split_axis=1, concat_axis=2, tiled=True), extra)
+        return (
+            jnp.concatenate(
+                lax.all_to_all(
+                    jnp.stack(jnp.split(result, lax.axis_size(HARM), axis=1)), HARM, 0, 0
+                ),
+                axis=2,
+            ),
+            extra,
+        )
 
     def operator(field):
         above, below = sides(field)

time: 379 us -> 526 us (1.39)
  local copies, waits for them, and re-layouts: 31.7 us -> 179 us
    unnamed x47 -> x287, local copies, waits for them, and re-layouts: 7.05 us -> 155 us
  transfers between devices with their start and end apart: 16 -> 16, of which waited for: 8 -> 8; matrix products, arithmetic and copies ran while one was open for 7% -> 12% of each run, Pallas kernels for 0% -> 0%
where the time goes in v1:
time: 526 us; the launch traced here: 525 us
  local copies, waits for them, and re-layouts  179 us (34%)
  blocking collectives  159 us (30%)
  starting transfers between devices  77.7 us (15%)
  waiting for transfers between devices  55.9 us (11%)
  other arithmetic  29.1 us (6%)
  between operations  16.3 us (3%)
  matrix products  7.86 us (1%)
    psum x16, blocking collectives, by_axis(): return functools.reduce(lax.psum, axes, shard)  159 us
    unnamed x287, local copies, waits for them, and re-layouts  155 us
    all_to_all x4, waiting for transfers between devices, across(): moved = lax.all_to_all(field, HARM, split_axis=2, concat_axis=1, tiled=True)  41.9 us
    all_to_all x4, starting transfers between devices, across(): moved = lax.all_to_all(field, HARM, split_axis=2, concat_axis=1, tiled=True)  29.3 us
    all_to_all x4, starting transfers between devices, across(): lax.all_to_all(jnp.stack(jnp.split(result, lax.axis_size(HARM), axis=1)),...  24.9 us
    all_to_all x4, waiting for transfers between devices, across(): lax.all_to_all(jnp.stack(jnp.split(result, lax.axis_size(HARM), axis=1)),...  13.9 us
    slice x18, local copies, waits for them, and re-layouts, stencil(): skewed = skewed + picked * jnp.roll(above, -amount, axis=3)  11.9 us
    ppermute x4, starting transfers between devices, extended(): lax.ppermute(head, axis, [((i + 1) % count, i) for i in range(ends)])  11.8 us
  transfers between devices with their start and end apart: 16, of which 8 were waited for; matrix products, arithmetic and copies ran while one was open for 12% of the time, Pallas kernels for 0%

profile of v1, /device:TPU:2, one launch (start us, length us, event | category | flops | bytes accessed | tf_op | source)
XLA Modules:
  0.0 524.5 jit_solution(14891315720565552888)
XLA Ops:
  9.1 12.2 %all-to-all-start = ((f32[2,2,128,128]{3,1,0,2:T(2,128)}), f32[2,2,128,128]{3,1,0,2:T(2,128)S(1)}, u32[]{:S(2)}, u32[]{:S(2)}) async-start(f32[2,2,128,128]{3,1,0,2:T(2,128)} %copy.395), calls=%async_computation | async-start | bytes 524288 | tf_op jit(solution)/shard_map/all_to_all | solution.py:139
  24.8 8.5 %all-to-all-done = f32[2,2,128,128]{3,1,0,2:T(2,128)S(1)} async-done(((f32[2,2,128,128]{3,1,0,2:T(2,128)}), f32[2,2,128,128]{3,1,0,2:T(2,128)S(1)}, u32[]{:S(2)}, u32[]{:S(2)}) %all-to-all-start) | async-done | bytes 262176 | tf_op jit(solution)/shard_map/all_to_all | solution.py:139
  72.4 6.0 %all-to-all-start.1 = ((f32[64,2,2,2,128]{4,3,2,1,0:T(2,128)}), f32[64,2,2,2,128]{4,3,2,1,0:T(2,128)S(1)}, u32[]{:S(2)}, u32[]{:S(2)}) async-start(f32[64,2,2,2,128]{4,3,2,1,0:T(2,128)} %constant_dynamic-update-slice_fusion), calls=%async_computation.1 | async-start | bytes 524288 | tf_op jit(solution)/shard_map/all_to_all | solution.py:143
  79.6 10.9 %all-to-all-done.1 = f32[64,2,2,2,128]{4,3,2,1,0:T(2,128)S(1)} async-done(((f32[64,2,2,2,128]{4,3,2,1,0:T(2,128)}), f32[64,2,2,2,128]{4,3,2,1,0:T(2,128)S(1)}, u32[]{:S(2)}, u32[]{:S(2)}) %all-to-all-start.1) | async-done | bytes 262176 | tf_op jit(solution)/shard_map/all_to_all | solution.py:143
  93.5 10.9 %psum.196 = f32[]{:T(128)} all-reduce(f32[]{:T(128)} %get-tuple-element.41), channel_id=1, replica_groups=mesh['harm_0'=4,'harm_1'=8,'harm_2'=2,'node'=4] {'harm_0'}, use_global_device_ids=true, to_apply=%region_1.2 | all-reduce | flops 1 | bytes 8 | tf_op jit(solution)/shard_map/psum | solution.py:35
  104.4 15.5 %psum.197 = f32[]{:T(128)} all-reduce(f32[]{:T(128)} %psum.196), channel_id=1, replica_groups=mesh['harm_0'=4,'harm_1'=8,'harm_2'=2,'node'=4] {'harm_1'}, use_global_device_ids=true, to_apply=%region_2.3 | all-reduce | flops 1 | bytes 8 | tf_op jit(solution)/shard_map/psum | solution.py:35
  123.0 9.2 %psum.199 = f32[]{:T(128)} all-reduce(f32[]{:T(128)} %psum.198), channel_id=1, replica_groups=mesh['harm_0'=4,'harm_1'=8,'harm_2'=2,'node'=4] {'node'}, use_global_device_ids=true, to_apply=%region_4.5 | all-reduce | flops 1 | bytes 8 | tf_op jit(solution)/shard_map/psum | solution.py:35
  136.4 5.7 %all-to-all-start.2 = ((f32[2,2,128,128]{3,1,0,2:T(2,128)}), f32[2,2,128,128]{3,1,0,2:T(2,128)S(1)}, u32[]{:S(2)}, u32[]{:S(2)}) async-start(f32[2,2,128,128]{3,1,0,2:T(2,128)} %copy.398), calls=%async_computation.2 | async-start | bytes 524288 | tf_op jit(solution)/shard_map/all_to_all | solution.py:139
  142.2 11.8 %all-to-all-done.2 = f32[2,2,128,128]{3,1,0,2:T(2,128)S(1)} async-done(((f32[2,2,128,128]{3,1,0,2:T(2,128)}), f32[2,2,128,128]{3,1,0,2:T(2,128)S(1)}, u32[]{:S(2)}, u32[]{:S(2)}) %all-to-all-start.2) | async-done | bytes 262176 | tf_op jit(solution)/shard_map/all_to_all | solution.py:139
  193.1 6.0 %all-to-all-start.3 = ((f32[64,2,2,2,128]{4,3,2,1,0:T(2,128)}), f32[64,2,2,2,128]{4,3,2,1,0:T(2,128)S(1)}, u32[]{:S(2)}, u32[]{:S(2)}) async-start(f32[64,2,2,2,128]{4,3,2,1,0:T(2,128)} %constant_dynamic-update-slice_fusion.64), calls=%async_computation.3 | async-start | bytes 524288 | tf_op jit(solution)/shard_map/all_to_all | solution.py:143
  214.6 11.0 %all-reduce.8 = (f32[]{:T(128)}, f32[1]{0:T(128)}) all-reduce(f32[]{:T(128)} %get-tuple-element.10, f32[1]{0:T(128)} %bitcast.152), channel_id=1, replica_groups=mesh['harm_0'=4,'harm_1'=8,'harm_2'=2,'node'=4] {'harm_0'}, use_global_device_ids=true, to_apply=%region_11.12 | all-reduce | flops 2 | bytes 16 | tf_op jit(solution)/shard_map/psum | solution.py:35
  225.6 17.0 %all-reduce.2 = (f32[]{:T(128)}, f32[1]{0:T(128)}) all-reduce(f32[]{:T(128)} %get-tuple-element.31, f32[1]{0:T(128)} %get-tuple-element.32), channel_id=1, replica_groups=mesh['harm_0'=4,'harm_1'=8,'harm_2'=2,'node'=4] {'harm_1'}, use_global_device_ids=true, to_apply=%region_12.13 | all-reduce | flops 2 | bytes 16 | tf_op jit(solution)/shard_map/psum | solution.py:35
  245.8 9.2 %all-reduce.5 = (f32[]{:T(128)}, f32[1]{0:T(128)}) all-reduce(f32[]{:T(128)} %get-tuple-element.37, f32[1]{0:T(128)} %get-tuple-element.38), channel_id=1, replica_groups=mesh['harm_0'=4,'harm_1'=8,'harm_2'=2,'node'=4] {'node'}, use_global_device_ids=true, to_apply=%region_14.15 | all-reduce | flops 2 | bytes 16 | tf_op jit(solution)/shard_map/psum | solution.py:35
  265.8 11.8 %all-to-all-done.4 = f32[2,2,128,128]{3,1,0,2:T(2,128)S(1)} async-done(((f32[2,2,128,128]{3,1,0,2:T(2,128)}), f32[2,2,128,128]{3,1,0,2:T(2,128)S(1)}, u32[]{:S(2)}, u32[]{:S(2)}) %all-to-all-start.4) | async-done | bytes 262176 | tf_op jit(solution)/shard_map/all_to_all | solution.py:139
  316.7 6.3 %all-to-all-start.5 = ((f32[64,2,2,2,128]{4,3,2,1,0:T(2,128)}), f32[64,2,2,2,128]{4,3,2,1,0:T(2,128)}, u32[]{:S(2)}, u32[]{:S(2)}) async-start(f32[64,2,2,2,128]{4,3,2,1,0:T(2,128)} %constant_dynamic-update-slice_fusion.128), calls=%async_computation.5 | async-start | bytes 524288 | tf_op jit(solution)/shard_map/all_to_all | solution.py:143
  340.4 11.0 %all-reduce.7 = (f32[]{:T(128)}, f32[2]{0:T(128)S(1)}) all-reduce(f32[]{:T(128)} %get-tuple-element.7, f32[2]{0:T(128)S(1)} %pad_maximum_fusion.22), channel_id=1, replica_groups=mesh['harm_0'=4,'harm_1'=8,'harm_2'=2,'node'=4] {'harm_0'}, use_global_device_ids=true, to_apply=%region_22.23 | all-reduce | flops 3 | bytes 24 | tf_op jit(solution)/shard_map/psum | solution.py:35
  351.4 17.6 %all-reduce.1 = (f32[]{:T(128)}, f32[2]{0:T(128)S(1)}) all-reduce(f32[]{:T(128)} %get-tuple-element.29, f32[2]{0:T(128)S(1)} %get-tuple-element.30), channel_id=1, replica_groups=mesh['harm_0'=4,'harm_1'=8,'harm_2'=2,'node'=4] {'harm_1'}, use_global_device_ids=true, to_apply=%region_23.24 | all-reduce | flops 3 | bytes 24 | tf_op jit(solution)/shard_map/psum | solution.py:35
  372.1 8.0 %all-reduce.4 = (f32[]{:T(128)}, f32[2]{0:T(128)S(1)}) all-reduce(f32[]{:T(128)} %get-tuple-element.35, f32[2]{0:T(128)S(1)} %get-tuple-element.36), channel_id=1, replica_groups=mesh['harm_0'=4,'harm_1'=8,'harm_2'=2,'node'=4] {'node'}, use_global_device_ids=true, to_apply=%region_25.26 | all-reduce | flops 3 | bytes 24 | tf_op jit(solution)/shard_map/psum | solution.py:35
  387.5 5.8 %all-to-all-start.6 = ((f32[2,2,128,128]{3,1,0,2:T(2,128)}), f32[2,2,128,128]{3,1,0,2:T(2,128)S(1)}, u32[]{:S(2)}, u32[]{:S(2)}) async-start(f32[2,2,128,128]{3,1,0,2:T(2,128)} %copy.404), calls=%async_computation.6 | async-start | bytes 524288 | tf_op jit(solution)/shard_map/all_to_all | solution.py:139
  395.5 9.7 %all-to-all-done.6 = f32[2,2,128,128]{3,1,0,2:T(2,128)S(1)} async-done(((f32[2,2,128,128]{3,1,0,2:T(2,128)}), f32[2,2,128,128]{3,1,0,2:T(2,128)S(1)}, u32[]{:S(2)}, u32[]{:S(2)}) %all-to-all-start.6) | async-done | bytes 262176 | tf_op jit(solution)/shard_map/all_to_all | solution.py:139
  444.4 6.5 %all-to-all-start.7 = ((f32[64,2,2,2,128]{4,3,2,1,0:T(2,128)}), f32[64,2,2,2,128]{4,3,2,1,0:T(2,128)}, u32[]{:S(2)}, u32[]{:S(2)}) async-start(f32[64,2,2,2,128]{4,3,2,1,0:T(2,128)} %constant_dynamic-update-slice_fusion.192), calls=%async_computation.7 | async-start | bytes 524288 | tf_op jit(solution)/shard_map/all_to_all | solution.py:143
  468.1 10.9 %all-reduce.6 = (f32[]{:T(128)}, f32[3]{0:T(128)S(1)}) all-reduce(f32[]{:T(128)} %get-tuple-element.3, f32[3]{0:T(128)S(1)} %pad_maximum_fusion.23), channel_id=1, replica_groups=mesh['harm_0'=4,'harm_1'=8,'harm_2'=2,'node'=4] {'harm_0'}, use_global_device_ids=true, to_apply=%region_35.36 | all-reduce | flops 4 | bytes 32 | tf_op jit(solution)/shard_map/psum | solution.py:35
  479.0 16.1 %all-reduce = (f32[]{:T(128)}, f32[3]{0:T(128)S(1)}) all-reduce(f32[]{:T(128)} %get-tuple-element.27, f32[3]{0:T(128)S(1)} %get-tuple-element.28), channel_id=1, replica_groups=mesh['harm_0'=4,'harm_1'=8,'harm_2'=2,'node'=4] {'harm_1'}, use_global_device_ids=true, to_apply=%region_36.37 | all-reduce | flops 4 | bytes 32 | tf_op jit(solution)/shard_map/psum | solution.py:35
  498.1 10.2 %all-reduce.3 = (f32[]{:T(128)}, f32[3]{0:T(128)S(1)}) all-reduce(f32[]{:T(128)} %get-tuple-element.33, f32[3]{0:T(128)S(1)} %get-tuple-element.34), channel_id=1, replica_groups=mesh['harm_0'=4,'harm_1'=8,'harm_2'=2,'node'=4] {'node'}, use_global_device_ids=true, to_apply=%region_38.39 | all-reduce | flops 4 | bytes 32 | tf_op jit(solution)/shard_map/psum | solution.py:35
  (430 shorter events, 260.2 us)
Async XLA Ops:
  1.4 23.2 %collective-permute-start = (f32[2,2,1,128]{3,2,1,0:T(1,128)S(1)}, f32[2,2,1,128]{3,2,1,0:T(1,128)S(1)}, u32[]{:S(2)}, u32[]{:S(2)}) collective-permute-start(f32[2,2,1,128]{3,2,1,0:T(1,128)S(1)} %get-tuple-element.69), channel_id=1, source_target_pairs={{0,1},{1,2},{2,3},{4,5},{5,6},{6,7},{8,9},{9,10},{10,11},{12,13},{... | collective-permute-start | bytes 6152 | tf_op jit(solution)/shard_map/ppermute | solution.py:25
  4.8 85.8 %collective-permute-start.1 = (f32[2,2,1,128]{3,2,1,0:T(1,128)S(1)}, f32[2,2,1,128]{3,2,1,0:T(1,128)S(1)}, u32[]{:S(2)}, u32[]{:S(2)}) collective-permute-start(f32[2,2,1,128]{3,2,1,0:T(1,128)S(1)} %get-tuple-element.70), channel_id=1, source_target_pairs={{1,0},{2,1},{3,2},{5,4},{6,5},{7,6},{9,8},{10,9},{11,10},{13,12},{... | collective-permute-start | bytes 6152 | tf_op jit(solution)/shard_map/ppermute | solution.py:27
  9.1 12.3 %copy-start.14 = (f32[3,4]{1,0:T(4,128)S(1)}, f32[3,4]{1,0:T(4,128)}, u32[]{:S(2)}) copy-start(f32[3,4]{1,0:T(4,128)} %param.12) | copy-start | bytes 148
  9.1 24.2 %all-to-all-start = ((f32[2,2,128,128]{3,1,0,2:T(2,128)}), f32[2,2,128,128]{3,1,0,2:T(2,128)S(1)}, u32[]{:S(2)}, u32[]{:S(2)}) async-start(f32[2,2,128,128]{3,1,0,2:T(2,128)} %copy.395), calls=%async_computation | async-start | bytes 524288 | tf_op jit(solution)/shard_map/all_to_all | solution.py:139
  21.3 1.6 copy-start
  72.4 18.0 %all-to-all-start.1 = ((f32[64,2,2,2,128]{4,3,2,1,0:T(2,128)}), f32[64,2,2,2,128]{4,3,2,1,0:T(2,128)S(1)}, u32[]{:S(2)}, u32[]{:S(2)}) async-start(f32[64,2,2,2,128]{4,3,2,1,0:T(2,128)} %constant_dynamic-update-slice_fusion), calls=%async_computation.1 | async-start | bytes 524288 | tf_op jit(solution)/shard_map/all_to_all | solution.py:143
  93.5 370.3 %copy-start.1 = (f32[2,2,128,128]{3,2,1,0:T(8,128)}, f32[2,2,128,128]{3,2,1,0:T(8,128)S(1)}, u32[]{:S(2)}) copy-start(f32[2,2,128,128]{3,2,1,0:T(8,128)S(1)} %get-tuple-element.42) | copy-start | bytes 786436
  136.4 17.6 %all-to-all-start.2 = ((f32[2,2,128,128]{3,1,0,2:T(2,128)}), f32[2,2,128,128]{3,1,0,2:T(2,128)S(1)}, u32[]{:S(2)}, u32[]{:S(2)}) async-start(f32[2,2,128,128]{3,1,0,2:T(2,128)} %copy.398), calls=%async_computation.2 | async-start | bytes 524288 | tf_op jit(solution)/shard_map/all_to_all | solution.py:139
  193.1 18.0 %all-to-all-start.3 = ((f32[64,2,2,2,128]{4,3,2,1,0:T(2,128)}), f32[64,2,2,2,128]{4,3,2,1,0:T(2,128)S(1)}, u32[]{:S(2)}, u32[]{:S(2)}) async-start(f32[64,2,2,2,128]{4,3,2,1,0:T(2,128)} %constant_dynamic-update-slice_fusion.64), calls=%async_computation.3 | async-start | bytes 524288 | tf_op jit(solution)/shard_map/all_to_all | solution.py:143
  199.2 7.0 %collective-permute-start.2 = (f32[2,2,1,128]{3,2,1,0:T(1,128)S(1)}, f32[2,2,1,128]{3,2,1,0:T(1,128)S(1)}, u32[]{:S(2)}, u32[]{:S(2)}) collective-permute-start(f32[2,2,1,128]{3,2,1,0:T(1,128)S(1)} %get-tuple-element.61), channel_id=1, source_target_pairs={{0,1},{1,2},{2,3},{4,5},{5,6},{6,7},{8,9},{9,10},{10,11},{12,13},{... | collective-permute-start | bytes 6152 | tf_op jit(solution)/shard_map/ppermute | solution.py:25
  203.2 8.0 %collective-permute-start.3 = (f32[2,2,1,128]{3,2,1,0:T(1,128)S(1)}, f32[2,2,1,128]{3,2,1,0:T(1,128)S(1)}, u32[]{:S(2)}, u32[]{:S(2)}) collective-permute-start(f32[2,2,1,128]{3,2,1,0:T(1,128)S(1)} %get-tuple-element.62), channel_id=1, source_target_pairs={{1,0},{2,1},{3,2},{5,4},{6,5},{7,6},{9,8},{10,9},{11,10},{13,12},{... | collective-permute-start | bytes 6152 | tf_op jit(solution)/shard_map/ppermute | solution.py:27
  260.0 17.6 %all-to-all-start.4 = ((f32[2,2,128,128]{3,1,0,2:T(2,128)}), f32[2,2,128,128]{3,1,0,2:T(2,128)S(1)}, u32[]{:S(2)}, u32[]{:S(2)}) async-start(f32[2,2,128,128]{3,1,0,2:T(2,128)} %copy.401), calls=%async_computation.4 | async-start | bytes 524288 | tf_op jit(solution)/shard_map/all_to_all | solution.py:139
  316.7 18.1 %all-to-all-start.5 = ((f32[64,2,2,2,128]{4,3,2,1,0:T(2,128)}), f32[64,2,2,2,128]{4,3,2,1,0:T(2,128)}, u32[]{:S(2)}, u32[]{:S(2)}) async-start(f32[64,2,2,2,128]{4,3,2,1,0:T(2,128)} %constant_dynamic-update-slice_fusion.128), calls=%async_computation.5 | async-start | bytes 524288 | tf_op jit(solution)/shard_map/all_to_all | solution.py:143
  323.0 6.8 %collective-permute-start.4 = (f32[2,2,1,128]{3,2,1,0:T(1,128)S(1)}, f32[2,2,1,128]{3,2,1,0:T(1,128)S(1)}, u32[]{:S(2)}, u32[]{:S(2)}) collective-permute-start(f32[2,2,1,128]{3,2,1,0:T(1,128)S(1)} %get-tuple-element.55), channel_id=1, source_target_pairs={{0,1},{1,2},{2,3},{4,5},{5,6},{6,7},{8,9},{9,10},{10,11},{12,13},{... | collective-permute-start | bytes 6152 | tf_op jit(solution)/shard_map/ppermute | solution.py:25
  326.1 9.9 %collective-permute-start.5 = (f32[2,2,1,128]{3,2,1,0:T(1,128)S(1)}, f32[2,2,1,128]{3,2,1,0:T(1,128)S(1)}, u32[]{:S(2)}, u32[]{:S(2)}) collective-permute-start(f32[2,2,1,128]{3,2,1,0:T(1,128)S(1)} %get-tuple-element.56), channel_id=1, source_target_pairs={{1,0},{2,1},{3,2},{5,4},{6,5},{7,6},{9,8},{10,9},{11,10},{13,12},{... | collective-permute-start | bytes 6152 | tf_op jit(solution)/shard_map/ppermute | solution.py:27
  334.8 1.1 copy-start.5
  334.8 1.1 copy-start.6
  387.5 17.8 %all-to-all-start.6 = ((f32[2,2,128,128]{3,1,0,2:T(2,128)}), f32[2,2,128,128]{3,1,0,2:T(2,128)S(1)}, u32[]{:S(2)}, u32[]{:S(2)}) async-start(f32[2,2,128,128]{3,1,0,2:T(2,128)} %copy.404), calls=%async_computation.6 | async-start | bytes 524288 | tf_op jit(solution)/shard_map/all_to_all | solution.py:139
  444.4 18.3 %all-to-all-start.7 = ((f32[64,2,2,2,128]{4,3,2,1,0:T(2,128)}), f32[64,2,2,2,128]{4,3,2,1,0:T(2,128)}, u32[]{:S(2)}, u32[]{:S(2)}) async-start(f32[64,2,2,2,128]{4,3,2,1,0:T(2,128)} %constant_dynamic-update-slice_fusion.192), calls=%async_computation.7 | async-start | bytes 524288 | tf_op jit(solution)/shard_map/all_to_all | solution.py:143
  450.9 6.7 %collective-permute-start.6 = (f32[2,2,1,128]{3,2,1,0:T(1,128)S(1)}, f32[2,2,1,128]{3,2,1,0:T(1,128)S(1)}, u32[]{:S(2)}, u32[]{:S(2)}) collective-permute-start(f32[2,2,1,128]{3,2,1,0:T(1,128)S(1)} %get-tuple-element.49), channel_id=1, source_target_pairs={{0,1},{1,2},{2,3},{4,5},{5,6},{6,7},{8,9},{9,10},{10,11},{12,13},{... | collective-permute-start | bytes 6152 | tf_op jit(solution)/shard_map/ppermute | solution.py:25
  454.1 9.8 %collective-permute-start.7 = (f32[2,2,1,128]{3,2,1,0:T(1,128)S(1)}, f32[2,2,1,128]{3,2,1,0:T(1,128)S(1)}, u32[]{:S(2)}, u32[]{:S(2)}) collective-permute-start(f32[2,2,1,128]{3,2,1,0:T(1,128)S(1)} %get-tuple-element.50), channel_id=1, source_target_pairs={{1,0},{2,1},{3,2},{5,4},{6,5},{7,6},{9,8},{10,9},{11,10},{13,12},{... | collective-permute-start | bytes 6152 | tf_op jit(solution)/shard_map/ppermute | solution.py:27
  460.0 3.8 copy-start.13
  462.7 1.1 copy-start.3
  462.7 1.1 copy-start.4
  (9 other events, 8.2 us)
